TPU v7x, 32 devices: a whole 2x2x4 slice. The times are simulated.
32 devices in a mesh: pod: 2 (over x), d: 16 (over z, y, core).
Axes of the slice: x: 2, y: 2, z: 4, core: 2. Of those that a mesh axis runs over, the one named last changes fastest.
Arguments:
- x: bfloat16 [32, 1024, 2048], P(('pod', 'd')), parts along dimension 0
- prompt_len: int32 [32], P(('pod', 'd')), parts along dimension 0
- ln_scale: float32 [2048], P('d')
- w_in: bfloat16 [2048, 18944], P('d')
- w_out: bfloat16 [10240, 2048], P(None, 'd')
Outputs:
- output 1: bfloat16 [32, 1024, 2048], P(('pod', 'd')), parts along dimension 0
- output 2: bfloat16 [32, 1024, 256], P(('pod', 'd')), parts along dimension 0
- output 3: bfloat16 [32, 1024, 256], P(('pod', 'd')), parts along dimension 0
There are 2 independent parts. A program takes and returns all parts, laid end to end along the dimension named above; an argument that names none is the same for every part.
All inputs are finite; a program needn't handle non-finite values.
Results may differ from a plain program's by a relative error of at most 0.00441177.
Values are sent between devices in bfloat16 or wider.
A program may use at most 1 GiB of HBM per device.

v0:
```python
import math
import jax
import jax.numpy as jnp
from jax import lax
from jax.sharding import PartitionSpec as P, NamedSharding

EPS = 1e-6
ROPE_BASE = 10000.0


def rope_tables(seq_len, head_dim):
    half_dim = head_dim // 2
    inv_freq = ROPE_BASE ** (-2.0 * jnp.arange(half_dim, dtype=jnp.float32) / head_dim)
    angles = jnp.arange(seq_len, dtype=jnp.float32)[:, None] * inv_freq[None, :]
    return jnp.cos(angles), jnp.sin(angles)


def apply_rope(rope_in, cos_b, sin_b):
    half_dim = rope_in.shape[-1] // 2
    lower_half = rope_in[..., :half_dim]
    upper_half = rope_in[..., half_dim:]
    return jnp.concatenate([lower_half * cos_b - upper_half * sin_b, upper_half * cos_b + lower_half * sin_b], axis=-1)


def layer_norm(x, ln_scale):
    x_float = x.astype(jnp.float32)
    centered = x_float - jnp.mean(x_float, axis=-1, keepdims=True)
    var_val = jnp.mean(centered * centered, axis=-1, keepdims=True)
    return (centered * lax.rsqrt(var_val + EPS) * ln_scale).astype(jnp.bfloat16)


def mix_tokens(projected, prompt_len, ffn_dim, attn_width, head_dim):
    num_seq = projected.shape[0]
    seq_len = projected.shape[1]
    num_heads = attn_width // head_dim
    q_start = 2 * ffn_dim
    k_start = q_start + attn_width
    v_start = k_start + head_dim
    gated = (jax.nn.silu(projected[..., :ffn_dim]) * projected[..., ffn_dim:q_start]).astype(jnp.bfloat16)
    cos_t, sin_t = rope_tables(seq_len, head_dim)
    q_rot = apply_rope(projected[..., q_start:k_start].reshape(num_seq, seq_len, num_heads, head_dim), cos_t[:, None, :], sin_t[:, None, :]).astype(jnp.bfloat16)
    k_rot = apply_rope(projected[..., k_start:v_start], cos_t, sin_t).astype(jnp.bfloat16)
    v_val = projected[..., v_start:].astype(jnp.bfloat16)
    scores = jnp.einsum("bthd,bsd->bths", q_rot, k_rot, preferred_element_type=jnp.float32) * (1.0 / math.sqrt(head_dim))
    positions = jnp.arange(seq_len)
    causal = positions[None, :] <= positions[:, None]
    valid_key = positions[None, :] < prompt_len[:, None]
    allowed = causal[None, :, None, :] & valid_key[:, None, None, :]
    probs_bf = jax.nn.softmax(jnp.where(allowed, scores, -1e30), axis=-1).astype(jnp.bfloat16)
    attn_out = jnp.einsum("bths,bsd->bthd", probs_bf, v_val, preferred_element_type=jnp.float32).astype(jnp.bfloat16)
    return gated, attn_out.reshape(num_seq, seq_len, attn_width), k_rot, v_val


def layer_math(x, prompt_len, ln_scale, w_in, w_out):
    model_width = x.shape[2]
    ffn_dim = 4 * model_width
    attn_width = w_out.shape[0] - ffn_dim
    head_dim = (w_in.shape[1] - 2 * ffn_dim - attn_width) // 2
    h_norm = layer_norm(x, ln_scale)
    projected = jnp.einsum("bte,ec->btc", h_norm, w_in, preferred_element_type=jnp.float32)
    gated, attn_out, k_rot, v_val = mix_tokens(projected, prompt_len, ffn_dim, attn_width, head_dim)
    out_sum = (jnp.einsum("btf,fe->bte", gated, w_out[:ffn_dim], preferred_element_type=jnp.float32)
               + jnp.einsum("btf,fe->bte", attn_out, w_out[ffn_dim:], preferred_element_type=jnp.float32))
    y_out = (x.astype(jnp.float32) + out_sum).astype(jnp.bfloat16)
    return y_out, k_rot, v_val


def solution(mesh):
    batch_spec = P(("pod", "d"))

    def local_layer(x, prompt_len, ln_shard, w_in_shard, w_out_shard):
        ln_scale = lax.all_gather(ln_shard, "d", axis=0, tiled=True)
        w_in = lax.all_gather(w_in_shard, "d", axis=0, tiled=True)
        w_out = lax.all_gather(w_out_shard, "d", axis=1, tiled=True)
        return layer_math(x, prompt_len, ln_scale, w_in, w_out)

    return jax.shard_map(local_layer, mesh=mesh,
                         in_specs=(batch_spec, batch_spec, P("d"), P("d", None), P(None, "d")),
                         out_specs=(batch_spec, batch_spec, batch_spec), check_vma=False)
```

profile of v0, /device:TPU:0, one launch (start us, length us, event | category | flops | bytes accessed | tf_op | source)
XLA Modules:
  0.0 671.6 jit_solution(595160494743325122)
XLA Ops:
  7.2 0.7 all-gather.4.cloned.1.call-update
  7.9 0.7 all-gather.6.cloned.1.call-update
  9.3 23.3 %all-gather = f32[16,1,128]{2,1,0:T(1,128)S(1)} all-gather(f32[1,1,128]{2,1,0:T(1,128)} %bitcast.47), channel_id=1, replica_groups=mesh['pod'=2,'d'=16] {'d'}, dimensions={0}, use_global_device_ids=true | all-gather | bytes 8704 | tf_op jit(solution)/shard_map/all_gather | solution.py:72
  32.6 2.8 convert_reduce_fusion
  35.4 3.4 fusion.13
  38.8 2.8 fusion.40
  41.7 1.3 fusion.30
  43.0 344.8 %all-gather.4.cloned.1.call-done = bf16[2048,18944]{1,0:T(8,128)(2,1)} async-done(((bf16[128,18944]{1,0:T(8,128)(2,1)}), bf16[2048,18944]{1,0:T(8,128)(2,1)}) %all-gather.4.cloned.1.call-update) | async-done | bytes 77594640 | tf_op jit(solution)/shard_map/all_gather | solution.py:73
  387.8 92.9 %convolution_bitcast_fusion = f32[1,1024,18944]{2,1,0:T(8,128)} fusion(bf16[2048,18944]{1,0:T(8,128)(2,1)} %all-gather.4.cloned.1.call-done, bf16[1,1024,2048]{2,1,0:T(8,128)(2,1)} %param.5, f32[2048]{0:T(1024)S(1)} %bitcast.46, f32[1024]{0:T(1024)S(1)} %add_rsqrt_fusion, f32[1024]{0:T(1024)S(1)} %broadcast_multiply_fusion), kind=kOutput, calls=%fused_computation.1 | convolution fusion | flops 79467380736 | bytes 159399936 | tf_op jit(solution)/shard_map/bte,ec->btc/dot_general | solution.py:60
  480.7 2.2 slice.75
  482.9 1.7 slice-done
  484.6 4.1 copy.21
  488.7 3.6 subtract_convert_fusion.1
  492.4 0.9 pad_maximum_fusion
  493.2 0.5 fusion.45
  493.8 0.5 copy-done.1
  494.3 0.2 copy-done.2
  494.4 1.6 fusion.32
  496.1 13.3 %fusion.23 = f32[1024,8,1024]{0,2,1:T(8,128)} fusion(bf16[1024,8,128]{2,0,1:T(8,128)(2,1)S(1)} %get-tuple-element.6, bf16[1024,8,128]{2,0,1:T(8,128)(2,1)S(1)} %get-tuple-element.5, bf16[1024,128]{1,0:T(8,128)(2,1)S(1)} %bitcast.45, bf16[1024,128]{1,0:T(8,128)(2,1)S(1)} %bitcast.44), kind=kOutput, calls=%fused_computation.27 | convolution fusion | flops 4304404480 | bytes 38273024 | tf_op jit(solution)/shard_map/bthd,bsd->bths/dot_general | solution.py:44
  509.4 33.5 %fusion.46 = (f32[1024,8]{0,1:T(8,128)S(1)}, f32[1024,8,1024]{0,2,1:T(8,128)}) fusion(f32[1024,8,1024]{0,2,1:T(8,128)} %fusion.23, pred[1024,1024]{0,1:T(8,128)(4,1)S(1)} %copy-done.3), kind=kOutput, calls=%fused_computation.64 | output fusion | flops 50332672 | bytes 68190208 | tf_op jit(solution)/shard_map/sub | solution.py:49
  542.8 15.8 %fusion.31 = bf16[1024,8,256]{0,2,1:T(8,128)(2,1)} fusion(f32[1024,8,1024]{0,2,1:T(8,128)} %get-tuple-element.12, f32[1024,8]{0,1:T(8,128)S(1)} %get-tuple-element.11, bf16[1,1024,256]{2,1,0:T(8,128)(2,1)S(1)} %copy-done.4), kind=kOutput, calls=%fused_computation.38 | convolution fusion | flops 4313841664 | bytes 38305792 | tf_op jit(solution)/shard_map/bths,bsd->bthd/dot_general | solution.py:50
  558.7 45.9 %all-gather.6.cloned.1.call-done = bf16[10240,2048]{1,0:T(8,128)(2,1)} async-done(((bf16[10240,128]{1,0:T(8,128)(2,1)}), bf16[10240,2048]{1,0:T(8,128)(2,1)}) %all-gather.6.cloned.1.call-update) | async-done | bytes 41943056 | tf_op jit(solution)/shard_map/all_gather | solution.py:74
  604.5 45.5 %fusion.1 = f32[1024,2048]{1,0:T(8,128)} fusion(bf16[10240,2048]{1,0:T(8,128)(2,1)} %all-gather.6.cloned.1.call-done, f32[1,1024,18944]{2,1,0:T(8,128)} %convolution_bitcast_fusion), kind=kOutput, calls=%fused_computation.2 | convolution fusion | flops 34410070016 | bytes 109051904 | tf_op jit(solution)/shard_map/btf,fe->bte/dot_general | solution.py:62
  650.1 14.7 %fusion.16 = bf16[1,1024,2048]{2,1,0:T(8,128)(2,1)} fusion(bf16[1,1024,2048]{2,1,0:T(8,128)(2,1)S(1)} %copy-done, f32[1024,2048]{1,0:T(8,128)} %fusion.1, bf16[1024,2048]{0,1:T(8,128)(2,1)S(1)} %bitcast.48, bf16[10240,2048]{1,0:T(8,128)(2,1)} %all-gather.6.cloned.1.call-done), kind=kOutput, calls=%fused_computation.23 | convolution fusion | flops 8598323200 | bytes 29360128 | tf_op jit(solution)/shard_map/btf,fe->bte/dot_general | solution.py:63
  (21 shorter events, 0.1 us)
Async XLA Ops:
  7.2 380.6 %all-gather.4.cloned.1.call-start = ((), (), s32[]{:S(2)}) async-start(), calls=%async_computation | async-start | bytes 82444288 | tf_op jit(solution)/shard_map/all_gather | solution.py:73
  7.9 596.6 %all-gather.6.cloned.1.call-start = ((), (), s32[]{:S(2)}) async-start(), calls=%async_computation.1 | async-start | bytes 44564480 | tf_op jit(solution)/shard_map/all_gather | solution.py:74
  32.6 6.3 copy-start.5
  480.7 3.9 slice-start
  484.6 4.1 copy-start.6
  493.2 1.0 copy-start.1
  493.2 1.2 copy-start.2
  496.0 13.3 %copy-start.3 = (pred[1024,1024]{0,1:T(8,128)(4,1)S(1)}, pred[1024,1024]{0,1:T(8,128)(4,1)}, u32[]{:S(2)}) copy-start(pred[1024,1024]{0,1:T(8,128)(4,1)} %fusion.30) | copy-start | bytes 3145732
  509.4 33.5 %copy-start.4 = (bf16[1,1024,256]{2,1,0:T(8,128)(2,1)S(1)}, bf16[1,1024,256]{2,1,0:T(8,128)(2,1)}, u32[]{:S(2)}) copy-start(bf16[1,1024,256]{2,1,0:T(8,128)(2,1)} %slice.75) | copy-start | bytes 1572868
  604.5 45.5 %copy-start = (bf16[1,1024,2048]{2,1,0:T(8,128)(2,1)S(1)}, bf16[1,1024,2048]{2,1,0:T(8,128)(2,1)}, u32[]{:S(2)}) copy-start(bf16[1,1024,2048]{2,1,0:T(8,128)(2,1)} %param.5) | copy-start | bytes 12582916
  604.5 45.5 %copy-start.7 = (bf16[1024,8,256]{0,2,1:T(8,128)(2,1)S(1)}, bf16[1024,8,256]{0,2,1:T(8,128)(2,1)}, u32[]{:S(2)}) copy-start(bf16[1024,8,256]{0,2,1:T(8,128)(2,1)} %fusion.31) | copy-start | bytes 12582916
Sparse Core Ops, SparseCore 0:
  9.6 378.1 all-gather.3
  389.3 215.2 all-gather.5
where the time goes:
time: 672 us
  waiting for transfers between devices  392 us (58%)
  matrix products  182 us (27%)
  other arithmetic  50 us (7%)
  blocking collectives  23.3 us (3%)
  between operations  14.8 us (2%)
  local copies, waits for them, and re-layouts  9.22 us (1%)
    all_gather x1, waiting for transfers between devices, local_layer(): w_in = lax.all_gather(w_in_shard, 'd', axis=0, tiled=True)  345 us
    dot_general x1, matrix products, layer_math(): jnp.einsum('bte,ec->btc', h_norm, w_in, preferred_element_type=jnp.float32)  92.9 us
    all_gather x1, waiting for transfers between devices, local_layer(): w_out = lax.all_gather(w_out_shard, 'd', axis=1, tiled=True)  45.9 us
    dot_general x1, matrix products, layer_math(): jnp.einsum('btf,fe->bte', gated, w_out[:ffn_dim], preferred_element_type=...  45.5 us
    sub x1, other arithmetic, mix_tokens(): jax.nn.softmax(jnp.where(allowed, scores, -1e+30), axis=-1)  33.5 us
    all_gather x1, blocking collectives, local_layer(): ln_scale = lax.all_gather(ln_shard, 'd', axis=0, tiled=True)  23.3 us
    dot_general x1, matrix products, mix_tokens(): jnp.einsum('bths,bsd->bthd', probs_bf, v_val, preferred_element_type=jnp....  15.8 us
    dot_general x1, matrix products, layer_math(): jnp.einsum('btf,fe->bte', attn_out, w_out[ffn_dim:], preferred_element_ty...  14.7 us
  transfers between devices with their start and end apart: 2, of which 2 were waited for; matrix products, arithmetic and copies ran while one was open for 27% of the time, Pallas kernels for 0%

commit v1 on v0

v1 whole, which is shorter than its diff:
```python
import functools
import math

import jax
import jax.numpy as jnp
import numpy as np
from jax import lax
from jax.experimental import pallas as pl
from jax.experimental.pallas import tpu as pltpu
from jax.sharding import PartitionSpec as P

MESH = pl.DeviceIdType.MESH
EPS = 1e-6
ROPE_BASE = 10000.0
E, F, HEADS, HEAD, T = 2048, 8192, 8, 256, 1024
Q0, K0 = 2 * F, 2 * F + HEADS * HEAD
UNIT = 512
TRIPLES = 19
NU = 3 * TRIPLES
M = 18
R = NU - M
LAG = 1
XLAG = 4
OFF = 4 * LAG + XLAG + 1
STEPS = 2 * TRIPLES + OFF + 1
RB = 256


def unit_of(s, pod):
    m, b = s // 2, s % 2
    return jnp.where(s < 2 * M, 3 * m + (1 - b) * pod + 2 * b, 3 * M + (s - 2 * M))


def device_of(r, c):
    y = r // 4
    z = (1 - y) * r + y * (7 - r)
    return (z * 2 + y) * 2 + c


def layer_kernel(x, plen, ln, w_in, w_out, cos, sin, y_out, k_out, v_out, G,
                 Pv, xv, h, acc, wg, wp, wx, wo, woa, a, q, kk, vv, o, cs, sn, ln_all,
                 pack_sem, own_sem, in_sem, out_sem, ld, rs, rr, xs, xr, ds_, dr, ls, lr):
    pod, d = lax.axis_index("pod"), lax.axis_index("d")
    c, yy, zz = d % 2, (d // 2) % 2, d // 4
    r = (1 - yy) * zz + yy * (7 - zz)
    right, left, partner = device_of((r + 1) % 8, c), device_of((r + 7) % 8, c), device_of(r, 1 - c)

    def pack_in(u, col):
        for j in range(4):
            pltpu.make_async_copy(w_in.at[:, pl.ds(pl.multiple_of(col + 128 * j, 128), 128)],
                                  Pv.at[u, pl.ds(128 * j, 128), :], pack_sem).start()

    def pack_out(u, row):
        pltpu.make_async_copy(w_out.at[pl.ds(row, UNIT), :], Pv.at[u], pack_sem).start()

    for u, col in ((0, K0), (1, Q0), (2, Q0 + 512), (3, Q0 + 1024), (4, Q0 + 1536)):
        pack_in(u, col)
    for i in range(4):
        pack_out(5 + i, F + UNIT * i)

    def pack_mlp(j, _):
        pack_in(9 + 3 * j, UNIT * j)
        pack_in(10 + 3 * j, F + UNIT * j)
        pack_out(11 + 3 * j, UNIT * j)
        return 0

    lax.fori_loop(0, TRIPLES - 3, pack_mlp, 0)
    x_in = pltpu.make_async_copy(x, xv, in_sem.at[0])
    cos_in = pltpu.make_async_copy(cos, cs, in_sem.at[1])
    sin_in = pltpu.make_async_copy(sin, sn, in_sem.at[2])
    x_in.start()
    cos_in.start()
    sin_in.start()

    bar = pltpu.get_barrier_semaphore()
    for t in range(1, 16):
        pl.semaphore_signal(bar, inc=1, device_id=(pod, (d + t) % 16), device_id_type=MESH)
    pl.semaphore_signal(bar, inc=1, device_id=(1 - pod, d), device_id_type=MESH)
    pltpu.make_async_copy(Pv, Pv, pack_sem).wait()
    own = pltpu.make_async_copy(Pv, G.at[:, c, 0], own_sem)
    own.start()
    pl.semaphore_wait(bar, 16)

    def ring(src, dst, s, e, to):
        return pltpu.make_async_remote_copy(src_ref=src, dst_ref=dst, send_sem=rs.at[s, e], recv_sem=rr.at[s, e],
                                            device_id=(pod, to), device_id_type=MESH)

    half0, half1 = pl.ds(0, 256), pl.ds(256, 256)

    def cw(s, hop):
        u = unit_of(s, pod)
        if hop == 1:
            return ring(Pv.at[u], G.at[u, c, 7], s, 0, right)
        if hop == 4:
            return ring(G.at[u, c, 5, half0], G.at[u, c, 4, half0], s, 6, right)
        return ring(G.at[u, c, 9 - hop], G.at[u, c, 8 - hop], s, 2 * (hop - 1), right)

    def ccw(s, hop):
        u = unit_of(s, pod)
        if hop == 1:
            return ring(Pv.at[u], G.at[u, c, 1], s, 1, left)
        if hop == 4:
            return ring(G.at[u, c, 3, half1], G.at[u, c, 4, half1], s, 7, left)
        return ring(G.at[u, c, hop - 1], G.at[u, c, hop], s, 2 * hop - 1, left)

    def cross(m, u):
        return pltpu.make_async_remote_copy(src_ref=G.at[u, c, pl.ds(1, 7)], dst_ref=G.at[u, c, pl.ds(1, 7)],
                                            send_sem=xs.at[m], recv_sem=xr.at[m],
                                            device_id=(1 - pod, d), device_id_type=MESH)

    def share(u, core):
        return pltpu.make_async_remote_copy(src_ref=G.at[u, core], dst_ref=G.at[u, core],
                                            send_sem=ds_.at[u], recv_sem=dr.at[u],
                                            device_id=(pod, partner), device_id_type=MESH)

    def ln_copy(t):
        return pltpu.make_async_remote_copy(src_ref=ln, dst_ref=ln_all.at[d], send_sem=ls.at[t], recv_sem=lr.at[t],
                                            device_id=(pod, (d + t) % 16), device_id_type=MESH)

    for t in range(1, 16):
        ln_copy(t).start()
    ln_all[pl.ds(d, 1)] = ln[...][None]

    def load_in(u, dst, sem):
        for j in range(4):
            pltpu.make_async_copy(G.at[u, :, :, pl.ds(128 * j, 128), :], dst.at[:, :, :, pl.ds(128 * j, 128)], sem).start()

    def load_out(u, dst, sem):
        for cc in range(2):
            for rel in range(8):
                src = device_of((r + rel) % 8, cc)
                pltpu.make_async_copy(G.at[u, cc, rel], dst.at[:, pl.ds(pl.multiple_of(src * 128, 128), 128)], sem).start()

    def wait_load(dst, sem):
        pltpu.make_async_copy(dst, dst, sem).wait()

    def rows(b):
        return pl.ds(b * RB, RB)

    def norm(b):
        xf = xv[rows(b), :].astype(jnp.float32)
        xc = xf - jnp.mean(xf, axis=-1, keepdims=True)
        xn = xc * lax.rsqrt(jnp.mean(xc * xc, axis=-1, keepdims=True) + EPS)
        for src in range(16):
            sc, sy, sz = src % 2, (src // 2) % 2, src // 4
            sr = (1 - sy) * sz + sy * (7 - sz)
            at = sc * 8 + (sr - r + 8) % 8
            h[rows(b), pl.ds(pl.multiple_of(at * 128, 128), 128)] = (
                xn[:, src * 128:(src + 1) * 128] * ln_all[src]).astype(jnp.bfloat16)
        acc[rows(b), :] = jnp.zeros((RB, E), jnp.float32)

    def proj(b, w):
        return jnp.dot(h[rows(b), :], w.reshape(E, UNIT), preferred_element_type=jnp.float32)

    def rope(b, u):
        lo, hi = u[:, :128], u[:, 128:]
        cb, sb = cs[rows(b), :], sn[rows(b), :]
        return jnp.concatenate([lo * cb - hi * sb, hi * cb + lo * sb], axis=-1).astype(jnp.bfloat16)

    def proj_kv(b, w):
        u = proj(b, w)
        kk[rows(b), :] = rope(b, u[:, :256])
        vv[rows(b), :] = u[:, 256:].astype(jnp.bfloat16)

    def proj_q(b, w, head):
        u = proj(b, w)
        q[head, rows(b), :] = rope(b, u[:, :256])
        q[head + 1, rows(b), :] = rope(b, u[:, 256:])

    def attend(b, head0):
        n = (b + 1) * RB
        qpos = b * RB + lax.broadcasted_iota(jnp.int32, (RB, n), 0)
        kpos = lax.broadcasted_iota(jnp.int32, (RB, n), 1)
        allowed = (kpos <= qpos) & (kpos < plen[0])

        def one(i, _):
            head = head0 + i
            s = lax.dot_general(q[head, rows(b), :], kk[0:n, :], (((1,), (1,)), ((), ())),
                                preferred_element_type=jnp.float32) * (1.0 / math.sqrt(HEAD))
            s = jnp.where(allowed, s, -1e30)
            e = jnp.exp(s - jnp.max(s, axis=-1, keepdims=True))
            p = (e * (1.0 / jnp.sum(e, axis=-1, keepdims=True))).astype(jnp.bfloat16)
            o[rows(b), pl.ds(pl.multiple_of(head * HEAD, HEAD), HEAD)] = jnp.dot(
                p, vv[0:n, :], preferred_element_type=jnp.float32).astype(jnp.bfloat16)
            return 0

        lax.fori_loop(0, 4, one, 0)

    def mlp_in(b, slot):
        g = proj(b, wg[slot])
        p = proj(b, wp[slot])
        a[rows(b), :] = (g * jax.nn.sigmoid(g) * p).astype(jnp.bfloat16)

    def y_copy(b):
        return pltpu.make_async_copy(xv.at[rows(b), :], y_out.at[rows(b), :], out_sem.at[b])

    k_copy = pltpu.make_async_copy(kk, k_out, out_sem.at[4])
    v_copy = pltpu.make_async_copy(vv, v_out, out_sem.at[5])

    def slice_in(b, t, slot):
        @pl.when(t == 0)
        def _():
            if b == 0:
                wait_load(wg.at[0], ld.at[0, 0])
                wait_load(wp.at[0], ld.at[0, 1])
            proj_kv(b, wg[0])
            proj_q(b, wp[0], 0)

        @pl.when(t == 1)
        def _():
            if b == 0:
                wait_load(wg.at[1], ld.at[1, 0])
            proj_q(b, wg[1], 4)

        @pl.when(t == 2)
        def _():
            if b == 0:
                k_copy.start()
                v_copy.start()
            attend(b, 0)

        @pl.when((t >= 3) & (t < TRIPLES))
        def _():
            if b == 0:
                wait_load(wg.at[slot], ld.at[slot, 0])
                wait_load(wp.at[slot], ld.at[slot, 1])
            mlp_in(b, slot)

        @pl.when((t >= 3) & (t < 7))
        def _():
            if b == 0:
                wait_load(woa, ld.at[0, 3])
            acc[rows(b), :] += jnp.dot(o[rows(b), pl.ds(pl.multiple_of((t - 3) * UNIT, UNIT), UNIT)], woa[...],
                                       preferred_element_type=jnp.float32)

    def slice_out(b, t, slot):
        @pl.when(t == 0)
        def _():
            if b == 0:
                wait_load(wx, ld.at[1, 3])
            proj_q(b, wx[...], 2)

        @pl.when(t == 1)
        def _():
            if b == 0:
                wait_load(wp.at[1], ld.at[1, 1])
            proj_q(b, wp[1], 6)

        @pl.when(t == 2)
        def _():
            attend(b, 4)

        @pl.when((t >= 3) & (t < TRIPLES))
        def _():
            if b == 0:
                wait_load(wo.at[slot], ld.at[slot, 2])
            acc[rows(b), :] += jnp.dot(a[rows(b), :], wo[slot], preferred_element_type=jnp.float32)

        @pl.when(t == TRIPLES - 1)
        def _():
            xv[rows(b), :] = (xv[rows(b), :].astype(jnp.float32) + acc[rows(b), :]).astype(jnp.bfloat16)
            if b:
                y_copy(b - 1).start()

    def arrive(t):
        @pl.when((t >= 0) & (t < TRIPLES))
        def _():
            for i in range(3):
                share(3 * t + i, 1 - c).wait_recv()
            slot = t % 2

            @pl.when(t == 0)
            def _():
                load_in(0, wg.at[0], ld.at[0, 0])
                load_in(1, wp.at[0], ld.at[0, 1])
                load_in(2, wx, ld.at[1, 3])

            @pl.when(t == 1)
            def _():
                load_in(3, wg.at[1], ld.at[1, 0])
                load_in(4, wp.at[1], ld.at[1, 1])

            @pl.when(t >= 3)
            def _():
                load_in(3 * t, wg.at[slot], ld.at[slot, 0])
                load_in(3 * t + 1, wp.at[slot], ld.at[slot, 1])
                load_out(3 * t + 2, wo.at[slot], ld.at[slot, 2])

            @pl.when((t >= 3) & (t < 7))
            def _():
                load_out(t + 2, woa, ld.at[0, 3])

    own.wait()

    def step(i, odd):
        is_out = odd == OFF % 2
        t = (i - OFF) // 2 - 1 if is_out else (i - OFF - 1) // 2
        t = jnp.where(i < OFF, -1, t)

        def work(b):
            (slice_out if is_out else slice_in)(b, t, t % 2)
            if not is_out:
                @pl.when(i == (2 if OFF % 2 else 3))
                def _():
                    if b == 0:
                        x_in.wait()
                        for j in range(1, 16):
                            ln_copy(j).wait_recv()
                        cos_in.wait()
                        sin_in.wait()
                    norm(b)

        @pl.when(i < R)
        def _():
            cw(i, 1).start()
            ccw(i, 1).start()

        for hop in (2, 3, 4):
            s = i - LAG * (hop - 1)

            @pl.when((s >= 0) & (s < R))
            def _():
                cw(s, hop - 1).wait_recv()
                cw(s, hop).start()
                ccw(s, hop - 1).wait_recv()
                ccw(s, hop).start()

            work(hop - 2)

        s = i - LAG * 4

        @pl.when((s >= 0) & (s < R))
        def _():
            cw(s, 4).wait_recv()
            ccw(s, 4).wait_recv()
            u = unit_of(s, pod)

            @pl.when((s < 2 * M) & (s % 2 == 0))
            def _():
                cross(s // 2, u).start()

            share(u, c).start()

        s = i - LAG * 4 - XLAG

        @pl.when((s >= 0) & (s < 2 * M) & (s % 2 == 0))
        def _():
            u = 3 * (s // 2) + 1 - pod
            cross(s // 2, u).wait_recv()
            share(u, c).start()

        work(3)
        if is_out:
            arrive(jnp.where(i < OFF, -1, (i - OFF) // 2))

    def two_steps(it, _):
        step(2 * it, 0)
        step(2 * it + 1, 1)
        return 0

    lax.fori_loop(0, (STEPS + 1) // 2, two_steps, 0)

    y_copy(3).start()
    for b in range(4):
        y_copy(b).wait()
    k_copy.wait()
    v_copy.wait()
    for t in range(1, 16):
        ln_copy(t).wait_send()

    def sent_units(u, _):
        share(u, c).wait_send()
        return 0

    def sent_ring(s, _):
        for hop in (1, 2, 3, 4):
            cw(s, hop).wait_send()
            ccw(s, hop).wait_send()
        return 0

    def sent_cross(m, _):
        cross(m, 3 * m + pod).wait_send()
        return 0

    lax.fori_loop(0, NU, sent_units, 0)
    lax.fori_loop(0, R, sent_ring, 0)
    lax.fori_loop(0, M, sent_cross, 0)


def layer(x, plen, ln, w_in, w_out, cos, sin):
    bf, f32 = jnp.bfloat16, jnp.float32
    anyspace = pl.BlockSpec(memory_space=pl.ANY)
    vmem = pltpu.VMEM
    dma = pltpu.SemaphoreType.DMA
    return pl.pallas_call(
        layer_kernel,
        name="layer",
        out_shape=(jax.ShapeDtypeStruct((T, E), bf), jax.ShapeDtypeStruct((T, HEAD), bf),
                   jax.ShapeDtypeStruct((T, HEAD), bf), jax.ShapeDtypeStruct((NU, 2, 8, UNIT, 128), bf)),
        in_specs=[anyspace, pl.BlockSpec(memory_space=pltpu.SMEM), pl.BlockSpec(memory_space=vmem),
                  anyspace, anyspace, anyspace, anyspace],
        out_specs=(anyspace,) * 4,
        scratch_shapes=[
            vmem((NU, UNIT, 128), bf), vmem((T, E), bf), vmem((T, E), bf), vmem((T, E), f32),
            vmem((2, 2, 8, 128, UNIT), bf), vmem((2, 2, 8, 128, UNIT), bf), vmem((2, 8, 128, UNIT), bf),
            vmem((2, UNIT, E), bf), vmem((UNIT, E), bf), vmem((T, UNIT), bf),
            vmem((HEADS, T, HEAD), bf), vmem((T, HEAD), bf), vmem((T, HEAD), bf), vmem((T, HEADS * HEAD), bf),
            vmem((T, 128), f32), vmem((T, 128), f32), vmem((16, 1, 128), f32),
            dma, dma, dma((3,)), dma((6,)), dma((2, 4)), dma((R, 8)), dma((R, 8)), dma((M,)), dma((M,)),
            dma((NU,)), dma((NU,)), dma((16,)), dma((16,))],
        compiler_params=pltpu.CompilerParams(collective_id=0, has_side_effects=True,
                                             vmem_limit_bytes=63 * 1024 * 1024),
    )(x, plen, ln, w_in, w_out, cos, sin)


def rope_tables():
    inv_freq = (ROPE_BASE ** (-2.0 * np.arange(HEAD // 2, dtype=np.float32) / HEAD)).astype(np.float32)
    angles = np.arange(T, dtype=np.float32)[:, None] * inv_freq[None, :]
    return np.cos(angles).astype(np.float32), np.sin(angles).astype(np.float32)


def solution(mesh):
    batch = P(("pod", "d"))
    cos, sin = rope_tables()

    def local_layer(x, plen, ln, w_in, w_out):
        y, k, v, _ = layer(x[0], plen, ln[None], w_in, w_out, cos, sin)
        return y[None], k[None], v[None]

    return jax.shard_map(local_layer, mesh=mesh,
                         in_specs=(batch, batch, P("d"), P("d", None), P(None, "d")),
                         out_specs=(batch, batch, batch), check_vma=False)
```

time: 672 us -> 448 us (0.67)
  Pallas kernels: 0 us -> 440 us
  waiting for transfers between devices: 392 us -> 0 us
  matrix products: 182 us -> 0 us
  other arithmetic: 50 us -> 0 us
  blocking collectives: 23.3 us -> 0 us
  between operations: 14.8 us -> 1.3 us
    pallas_call x0 -> x1, Pallas kernels: none -> 440 us  [layer(): pl.pallas_call(layer_kernel, name='layer', out_shape=(jax.ShapeDtypeStruc...]
    all_gather x2 -> x0, waiting for transfers between devices: 391 us -> none  [the longest x1 345 us: local_layer(): w_in = lax.all_gather(w_in_shard, 'd', axis=0, tiled=True)]
    dot_general x5 -> x0, matrix products: 182 us -> none  [the longest x1 92.9 us: layer_math(): jnp.einsum('bte,ec->btc', h_norm, w_in, preferred_element_type=jnp.float32)]
    sub x1 -> x0, other arithmetic: 33.5 us -> none  [mix_tokens(): jax.nn.softmax(jnp.where(allowed, scores, -1e+30), axis=-1)]
    all_gather x1 -> x0, blocking collectives: 23.3 us -> none  [local_layer(): ln_scale = lax.all_gather(ln_shard, 'd', axis=0, tiled=True)]
  transfers between devices with their start and end apart: 2 -> 0, of which waited for: 2 -> 0; matrix products, arithmetic and copies ran while one was open for 27% -> 0% of each run, Pallas kernels for 0% -> 0%
where the time goes in v1:
time: 448 us
  Pallas kernels  440 us (98%)
  local copies, waits for them, and re-layouts  6.47 us (1%)
    pallas_call x1, Pallas kernels, layer(): pl.pallas_call(layer_kernel, name='layer', out_shape=(jax.ShapeDtypeStruc...  440 us

profile of v1, /device:TPU:0, one launch (start us, length us, event | category | flops | bytes accessed | tf_op | source)
XLA Modules:
  0.0 447.6 jit_solution(17556902844176009889)
XLA Ops:
  1.3 439.8 %layer.1 = (bf16[1024,2048]{1,0:T(8,128)(2,1)}, bf16[1024,256]{1,0:T(8,128)(2,1)}, bf16[1024,256]{1,0:T(8,128)(2,1)}, bf16[57,2,8,512,128]{4,3,2,1,0:T(8,128)(2,1)}) custom-call(bf16[1024,2048]{1,0:T(8,128)(2,1)} %bitcast.5, s32[1]{0:T(128)S(6)} %copy.13.plen, f32[1,128]{1,0:T(1,128)} %bitcast.9, bf16[128,18944]{1,0:T(8,128)(2,1)} %w_in.1, ...), custom_call_target="tpu_custom_call" | custom-call | tf_op jit(solution)/shard_map/layer/pallas_call | solution.py:395
  441.1 0.0 copy-start.1
  441.1 0.0 copy-start
  441.1 4.9 %copy.14 = bf16[1,1024,2048]{2,1,0:T(8,128)(2,1)} copy(bf16[1,1024,2048]{2,1,0:T(8,128)(2,1)} %bitcast.6) | data formatting | bytes 8388608
  446.0 0.0 copy-done.1
  446.0 0.8 copy.15
  446.8 0.0 copy-done
  446.8 0.8 copy.16
Async XLA Ops:
  441.1 4.9 %copy-start.1 = (bf16[1024,256]{1,0:T(8,128)(2,1)S(1)}, bf16[1024,256]{1,0:T(8,128)(2,1)}, u32[]{:S(2)}) copy-start(bf16[1024,256]{1,0:T(8,128)(2,1)} %get-tuple-element.7) | copy-start | bytes 1572868
  441.1 5.7 %copy-start = (bf16[1024,256]{1,0:T(8,128)(2,1)S(1)}, bf16[1024,256]{1,0:T(8,128)(2,1)}, u32[]{:S(2)}) copy-start(bf16[1024,256]{1,0:T(8,128)(2,1)} %get-tuple-element.8) | copy-start | bytes 1572868

commit v2 on v1

v2 whole, which is shorter than its diff:
```python
import functools
import math

import jax
import jax.numpy as jnp
import numpy as np
from jax import lax
from jax.experimental import pallas as pl
from jax.experimental.pallas import tpu as pltpu
from jax.sharding import PartitionSpec as P

MESH = pl.DeviceIdType.MESH
EPS = 1e-6
ROPE_BASE = 10000.0
E, F, HEADS, HEAD, T = 2048, 8192, 8, 256, 1024
Q0, K0 = 2 * F, 2 * F + HEADS * HEAD
UNIT = 512
TRIPLES = 19
NU = 3 * TRIPLES
LAST = TRIPLES - 1
M = 18
R = NU - M
LAG = 1
XLAG = 1
OFF = 4 * LAG + XLAG + 1
STEPS = 2 * LAST + OFF + 2
DONE = 8
RB = 256


def unit_of(s, pod):
    m, b = s // 2, s % 2
    return jnp.where(s < 2 * M, 3 * m + (1 - b) * pod + 2 * b, 3 * M + (s - 2 * M))


def device_of(r, c):
    y = r // 4
    z = (1 - y) * r + y * (7 - r)
    return (z * 2 + y) * 2 + c


def layer_kernel(x, plen, ln, w_in, w_out, tab, y_out, k_out, v_out, G,
                 Pv, xv, h, acc, wg, wp, wx, wo, woa, a, q, kk, vv, o, cs, sn, tb, ln_all,
                 pack_sem, own_sem, in_sem, out_sem, ld, rs, rr, xs, xr, ds_, dr, ls, lr):
    pod, d = lax.axis_index("pod"), lax.axis_index("d")
    c, yy, zz = d % 2, (d // 2) % 2, d // 4
    r = (1 - yy) * zz + yy * (7 - zz)
    right, left, partner = device_of((r + 1) % 8, c), device_of((r + 7) % 8, c), device_of(r, 1 - c)

    def pack_in(u, col, first=1):
        for j in range(4):
            pltpu.make_async_copy(w_in.at[:, pl.ds(pl.multiple_of(col + 128 * j, 128), 128)],
                                  Pv.at[u, pl.ds(128 * j, 128), :], pack_sem.at[first]).start()

    def pack_out(u, row):
        pltpu.make_async_copy(w_out.at[pl.ds(row, UNIT), :], Pv.at[u], pack_sem.at[1]).start()

    for u, col in ((0, K0), (1, Q0), (2, Q0 + 512)):
        pack_in(u, col, 0)
    bar = pltpu.get_barrier_semaphore()
    for t in range(1, 16):
        pl.semaphore_signal(bar, inc=1, device_id=(pod, (d + t) % 16), device_id_type=MESH)
    pl.semaphore_signal(bar, inc=1, device_id=(1 - pod, d), device_id_type=MESH)
    x_in = pltpu.make_async_copy(x, xv, in_sem.at[0])
    tab_in = pltpu.make_async_copy(tab, tb, in_sem.at[1])
    own = pltpu.make_async_copy(Pv, G.at[:, c, 0], own_sem)
    pltpu.make_async_copy(Pv.at[pl.ds(0, 3)], Pv.at[pl.ds(0, 3)], pack_sem.at[0]).wait()
    pl.semaphore_wait(bar, 16)

    def ring(src, dst, s, e, to):
        return pltpu.make_async_remote_copy(src_ref=src, dst_ref=dst, send_sem=rs.at[s, e], recv_sem=rr.at[s, e],
                                            device_id=(pod, to), device_id_type=MESH)

    half0, half1 = pl.ds(0, 256), pl.ds(256, 256)

    def cw(s, hop):
        u = unit_of(s, pod)
        if hop == 1:
            return ring(Pv.at[u], G.at[u, c, 7], s, 0, right)
        if hop == 4:
            return ring(G.at[u, c, 5, half0], G.at[u, c, 4, half0], s, 6, right)
        return ring(G.at[u, c, 9 - hop], G.at[u, c, 8 - hop], s, 2 * (hop - 1), right)

    def ccw(s, hop):
        u = unit_of(s, pod)
        if hop == 1:
            return ring(Pv.at[u], G.at[u, c, 1], s, 1, left)
        if hop == 4:
            return ring(G.at[u, c, 3, half1], G.at[u, c, 4, half1], s, 7, left)
        return ring(G.at[u, c, hop - 1], G.at[u, c, hop], s, 2 * hop - 1, left)

    def cross(m, u, at, n):
        return pltpu.make_async_remote_copy(src_ref=G.at[u, c, pl.ds(at, n)], dst_ref=G.at[u, c, pl.ds(at, n)],
                                            send_sem=xs.at[m], recv_sem=xr.at[m],
                                            device_id=(1 - pod, d), device_id_type=MESH)

    def share(u, core, at=0, n=8, src=None):
        here = G.at[u, core, pl.ds(at, n)]
        return pltpu.make_async_remote_copy(src_ref=here if src is None else src, dst_ref=here,
                                            send_sem=ds_.at[u], recv_sem=dr.at[u],
                                            device_id=(pod, partner), device_id_type=MESH)

    def pass_on(s, at):
        u = unit_of(s, pod)

        @pl.when((s < 2 * M) & (s % 2 == 0))
        def _():
            cross(s // 2, u, at, 1).start()

        share(u, c, at, 1).start()

    def ln_copy(t):
        return pltpu.make_async_remote_copy(src_ref=ln, dst_ref=ln_all.at[d], send_sem=ls.at[t], recv_sem=lr.at[t],
                                            device_id=(pod, (d + t) % 16), device_id_type=MESH)

    def send_own(s):
        cw(s, 1).start()
        ccw(s, 1).start()
        u = unit_of(s, pod)
        share(u, c, 0, 1, Pv.at[pl.ds(u, 1)]).start()

    send_own(0)
    for t in range(1, 16):
        ln_copy(t).start()
    ln_all[pl.ds(d, 1)] = ln[...][None]
    x_in.start()
    tab_in.start()
    for u, col in ((3, Q0 + 1024), (4, Q0 + 1536)):
        pack_in(u, col)
    pack_out(5, F)
    for i in range(3):
        pack_out(3 * LAST + i, F + UNIT * (i + 1))

    def pack_mlp(j, _):
        pack_in(6 + 3 * j, UNIT * j)
        pack_in(7 + 3 * j, F + UNIT * j)
        pack_out(8 + 3 * j, UNIT * j)
        return 0

    lax.fori_loop(0, F // UNIT, pack_mlp, 0)

    def load_in(u, dst, sem):
        for j in range(4):
            pltpu.make_async_copy(G.at[u, :, :, pl.ds(128 * j, 128), :], dst.at[:, :, :, pl.ds(128 * j, 128)], sem).start()

    def load_out(u, dst, sem):
        for cc in range(2):
            for rel in range(8):
                src = device_of((r + rel) % 8, cc)
                pltpu.make_async_copy(G.at[u, cc, rel], dst.at[:, pl.ds(pl.multiple_of(src * 128, 128), 128)], sem).start()

    def wait_load(dst, sem):
        pltpu.make_async_copy(dst, dst, sem).wait()

    def rows(b):
        return pl.ds(b * RB, RB)

    def norm(b):
        xf = xv[rows(b), :].astype(jnp.float32)
        xc = xf - jnp.mean(xf, axis=-1, keepdims=True)
        xn = xc * lax.rsqrt(jnp.mean(xc * xc, axis=-1, keepdims=True) + EPS)
        for src in range(16):
            sc, sy, sz = src % 2, (src // 2) % 2, src // 4
            sr = (1 - sy) * sz + sy * (7 - sz)
            at = sc * 8 + (sr - r + 8) % 8
            h[rows(b), pl.ds(pl.multiple_of(at * 128, 128), 128)] = (
                xn[:, src * 128:(src + 1) * 128] * ln_all[src]).astype(jnp.bfloat16)
        acc[rows(b), :] = xf

    def tables(b):
        cb, sb = tb[2], tb[3]
        for i in range(RB // 32):
            n = b * (RB // 32) + i
            ca, sa = tb[0, n:n + 1, :], tb[1, n:n + 1, :]
            cs[pl.ds(32 * n, 32), :] = ca * cb - sa * sb
            sn[pl.ds(32 * n, 32), :] = sa * cb + ca * sb

    def proj(b, w):
        return jnp.dot(h[rows(b), :], w.reshape(E, UNIT), preferred_element_type=jnp.float32)

    def rope(b, u):
        lo, hi = u[:, :128], u[:, 128:]
        cb, sb = cs[rows(b), :], sn[rows(b), :]
        return jnp.concatenate([lo * cb - hi * sb, hi * cb + lo * sb], axis=-1).astype(jnp.bfloat16)

    def proj_kv(b, w):
        u = proj(b, w)
        kk[rows(b), :] = rope(b, u[:, :256])
        vv[rows(b), :] = u[:, 256:].astype(jnp.bfloat16)

    def proj_q(b, w, head):
        u = proj(b, w)
        q[head, rows(b), :] = rope(b, u[:, :256])
        q[head + 1, rows(b), :] = rope(b, u[:, 256:])

    def attend(b, head):
        n = (b + 1) * RB
        qpos = b * RB + lax.broadcasted_iota(jnp.int32, (RB, n), 0)
        kpos = lax.broadcasted_iota(jnp.int32, (RB, n), 1)
        allowed = (kpos <= qpos) & (kpos < plen[0])

        s = lax.dot_general(q[head, rows(b), :], kk[0:n, :], (((1,), (1,)), ((), ())),
                            preferred_element_type=jnp.float32) * (1.0 / math.sqrt(HEAD))
        s = jnp.where(allowed, s, -1e30)
        e = jnp.exp(s - jnp.max(s, axis=-1, keepdims=True))
        p = (e * (1.0 / jnp.sum(e, axis=-1, keepdims=True))).astype(jnp.bfloat16)
        o[rows(b), pl.ds(pl.multiple_of(head * HEAD, HEAD), HEAD)] = jnp.dot(
            p, vv[0:n, :], preferred_element_type=jnp.float32).astype(jnp.bfloat16)

    def mlp_in(b, slot):
        g = proj(b, wg[slot])
        p = proj(b, wp[slot])
        a[rows(b), :] = (g * jax.nn.sigmoid(g) * p).astype(jnp.bfloat16)

    def y_copy(b):
        return pltpu.make_async_copy(xv.at[rows(b), :], y_out.at[rows(b), :], out_sem.at[b])

    k_copy = pltpu.make_async_copy(kk, k_out, out_sem.at[4])
    v_copy = pltpu.make_async_copy(vv, v_out, out_sem.at[5])

    def slice_in(b, t, slot):
        @pl.when(t == 0)
        def _():
            if b == 0:
                wait_load(wg.at[0], ld.at[0, 0])
                wait_load(wp.at[0], ld.at[0, 1])
            proj_kv(b, wg[0])
            proj_q(b, wp[0], 0)

        @pl.when(t == 1)
        def _():
            if b == 0:
                wait_load(wg.at[1], ld.at[1, 0])
            proj_q(b, wg[1], 4)

        @pl.when((t >= 2) & (t < LAST))
        def _():
            if b == 0:
                wait_load(wg.at[slot], ld.at[slot, 0])
                wait_load(wp.at[slot], ld.at[slot, 1])
            mlp_in(b, slot)

    def slice_out(b, t, slot):
        @pl.when(t == 0)
        def _():
            if b == 0:
                wait_load(wx, ld.at[1, 3])
            proj_q(b, wx[...], 2)

        @pl.when(t == 1)
        def _():
            if b == 0:
                wait_load(wp.at[1], ld.at[1, 1])
            proj_q(b, wp[1], 6)

        @pl.when((t >= 2) & (t < LAST))
        def _():
            if b == 0:
                wait_load(wo.at[slot], ld.at[slot, 2])
            acc[rows(b), :] += jnp.dot(a[rows(b), :], wo[slot], preferred_element_type=jnp.float32)

    def out_attention(b, i, w):
        return acc[rows(b), :] + jnp.dot(o[rows(b), i * UNIT:(i + 1) * UNIT], w[...], preferred_element_type=jnp.float32)

    def attention(blocks, t, second):
        @pl.when((t >= 2) & (t < 2 + HEADS // 2))
        def _():
            for b in blocks:
                attend(b, 2 * (t - 2) + second)

    def here(u):
        share(u, 1 - c).wait_recv()

    def arrive(t):
        slot = t % 2

        @pl.when((t >= 0) & (t < LAST))
        def _():
            for i in range(3):
                here(3 * t + i)

        @pl.when(t == 0)
        def _():
            load_in(0, wg.at[0], ld.at[0, 0])
            load_in(1, wp.at[0], ld.at[0, 1])
            load_in(2, wx, ld.at[1, 3])

        @pl.when(t == 1)
        def _():
            load_in(3, wg.at[1], ld.at[1, 0])
            load_in(4, wp.at[1], ld.at[1, 1])

        @pl.when((t >= 2) & (t < LAST))
        def _():
            load_in(3 * t, wg.at[slot], ld.at[slot, 0])
            load_in(3 * t + 1, wp.at[slot], ld.at[slot, 1])
            load_out(3 * t + 2, wo.at[slot], ld.at[slot, 2])

        @pl.when(t == 6)
        def _():
            load_out(5, woa, ld.at[0, 3])

        @pl.when(t == LAST)
        def _():
            here(3 * LAST + 1)
            load_out(3 * LAST + 1, wo.at[LAST % 2], ld.at[LAST % 2, 2])

    def step(i, odd):
        is_out = odd == OFF % 2
        t = jnp.where(i < OFF, -1, (i - OFF) // 2)
        slot = t % 2

        def work(n):
            if is_out:
                before = jnp.where(i < OFF, -1, t - 1)
                if n < 2:
                    slice_out(2 * n, before, (t + 1) % 2)
                    slice_out(2 * n + 1, before, (t + 1) % 2)
                    if n == 1:
                        arrive(t)
                elif n == 2:
                    attention((0, 1, 2), t, 0)

                    @pl.when(t == LAST)
                    def _():
                        wait_load(woa, ld.at[0, 3])
                        for b in range(4):
                            acc[rows(b), :] = out_attention(b, 1, woa)
                else:
                    slice_in(0, t, slot)
                    attention((3,), t, 0)
                return
            if n == 0:
                @pl.when(i == (2 if OFF % 2 else 3))
                def _():
                    x_in.wait()
                    for j in range(1, 16):
                        ln_copy(j).wait_recv()
                    tab_in.wait()

                @pl.when(t == 2)
                def _():
                    k_copy.start()
                    v_copy.start()

            @pl.when(i == (2 if OFF % 2 else 3))
            def _():
                norm(n)
                tables(n)

            if n < 3:
                slice_in(n + 1, t, slot)
            attention(((0, 1), (2,), (), (3,))[n], t, 1)
            if n == 3:
                @pl.when(t == 6)
                def _():
                    wait_load(woa, ld.at[0, 3])
                    for b in range(4):
                        acc[rows(b), :] = out_attention(b, 0, woa)

                @pl.when(t == LAST - 1)
                def _():
                    here(3 * LAST)
                    load_out(3 * LAST, woa, ld.at[0, 3])

        @pl.when(i == 2)
        def _():
            pltpu.make_async_copy(Pv.at[pl.ds(3, NU - 3)], Pv.at[pl.ds(3, NU - 3)], pack_sem.at[1]).wait()
            own.start()

        @pl.when(i == 4)
        def _():
            own.wait()

        @pl.when((i > 0) & (i < R))
        def _():
            send_own(i)

        for hop in (2, 3, 4):
            s = i - LAG * (hop - 1)

            @pl.when((s >= 0) & (s < R))
            def _():
                cw(s, hop - 1).wait_recv()
                cw(s, hop).start()
                pass_on(s, 9 - hop)
                ccw(s, hop - 1).wait_recv()
                ccw(s, hop).start()
                pass_on(s, hop - 1)

            work(hop - 2)

        s = i - LAG * 4

        @pl.when((s >= 0) & (s < R))
        def _():
            cw(s, 4).wait_recv()
            ccw(s, 4).wait_recv()
            pass_on(s, 4)

        s = i - LAG * 4 - XLAG

        @pl.when((s >= 0) & (s < 2 * M) & (s % 2 == 0))
        def _():
            u = 3 * (s // 2) + 1 - pod
            cross(s // 2, u, 1, 7).wait_recv()
            share(u, c).start()

        work(3)
        s = i - DONE

        @pl.when((s >= 0) & (s < R))
        def _():
            sent(s)

    def sent(s):
        for hop in (1, 2, 3, 4):
            cw(s, hop).wait_send()
            ccw(s, hop).wait_send()
        share(unit_of(s, pod), c).wait_send()

        @pl.when((s < 2 * M) & (s % 2 == 0))
        def _():
            m = s // 2
            cross(m, 3 * m + pod, 1, 7).wait_send()
            share(3 * m + 1 - pod, c).wait_send()

    def two_steps(it, _):
        step(2 * it, 0)
        step(2 * it + 1, 1)
        return 0

    lax.fori_loop(0, STEPS // 2, two_steps, 0)

    last = LAST % 2
    wait_load(wo.at[last], ld.at[last, 2])
    for b in range(4):
        if b == 2:
            here(3 * LAST + 2)
            load_out(3 * LAST + 2, wo.at[1 - last], ld.at[1 - last, 2])
        acc[rows(b), :] = out_attention(b, 2, wo.at[last])
    wait_load(wo.at[1 - last], ld.at[1 - last, 2])
    for b in range(4):
        xv[rows(b), :] = out_attention(b, 3, wo.at[1 - last]).astype(jnp.bfloat16)
        if b:
            y_copy(b - 1).start()
    y_copy(3).start()

    def sent_late(s, _):
        sent(s)
        return 0

    lax.fori_loop(STEPS - DONE, R, sent_late, 0)
    for t in range(1, 16):
        ln_copy(t).wait_send()
    for b in range(4):
        y_copy(b).wait()
    k_copy.wait()
    v_copy.wait()


def layer(x, plen, ln, w_in, w_out, tab):
    bf, f32 = jnp.bfloat16, jnp.float32
    anyspace = pl.BlockSpec(memory_space=pl.ANY)
    vmem = pltpu.VMEM
    dma = pltpu.SemaphoreType.DMA
    return pl.pallas_call(
        layer_kernel,
        name="layer",
        out_shape=(jax.ShapeDtypeStruct((T, E), bf), jax.ShapeDtypeStruct((T, HEAD), bf),
                   jax.ShapeDtypeStruct((T, HEAD), bf), jax.ShapeDtypeStruct((NU, 2, 8, UNIT, 128), bf)),
        in_specs=[anyspace, pl.BlockSpec(memory_space=pltpu.SMEM), pl.BlockSpec(memory_space=vmem),
                  anyspace, anyspace, anyspace],
        out_specs=(anyspace,) * 4,
        scratch_shapes=[
            vmem((NU, UNIT, 128), bf), vmem((T, E), bf), vmem((T, E), bf), vmem((T, E), f32),
            vmem((2, 2, 8, 128, UNIT), bf), vmem((2, 2, 8, 128, UNIT), bf), vmem((2, 8, 128, UNIT), bf),
            vmem((2, UNIT, E), bf), vmem((UNIT, E), bf), vmem((T, UNIT), bf),
            vmem((HEADS, T, HEAD), bf), vmem((T, HEAD), bf), vmem((T, HEAD), bf), vmem((T, HEADS * HEAD), bf),
            vmem((T, 128), f32), vmem((T, 128), f32), vmem((4, 32, 128), f32), vmem((16, 1, 128), f32),
            dma((2,)), dma, dma((2,)), dma((6,)), dma((2, 4)), dma((R, 8)), dma((R, 8)), dma((M,)), dma((M,)),
            dma((NU,)), dma((NU,)), dma((16,)), dma((16,))],
        compiler_params=pltpu.CompilerParams(collective_id=0, has_side_effects=True,
                                             vmem_limit_bytes=63 * 1024 * 1024),
    )(x, plen, ln, w_in, w_out, tab)


def rope_tables():
    freq = ROPE_BASE ** (-2.0 * np.arange(HEAD // 2) / HEAD)
    fine = np.arange(32)[:, None] * freq[None, :]
    return np.stack([np.cos(32 * fine), np.sin(32 * fine), np.cos(fine), np.sin(fine)]).astype(np.float32)


def solution(mesh):
    batch = P(("pod", "d"))
    tab = rope_tables()

    def local_layer(x, plen, ln, w_in, w_out):
        y, k, v, _ = layer(x[0], plen, ln[None], w_in, w_out, tab)
        return y[None], k[None], v[None]

    return jax.shard_map(local_layer, mesh=mesh,
                         in_specs=(batch, batch, P("d"), P("d", None), P(None, "d")),
                         out_specs=(batch, batch, batch), check_vma=False)
```

time: 448 us -> 420 us (0.938)
  Pallas kernels: 440 us -> 412 us
    pallas_call x1, Pallas kernels: 440 us -> 412 us  [layer(): pl.pallas_call(layer_kernel, name='layer', out_shape=(jax.ShapeDtypeStruc...]
where the time goes in v2:
time: 420 us
  Pallas kernels  412 us (98%)
  local copies, waits for them, and re-layouts  6.47 us (2%)
    pallas_call x1, Pallas kernels, layer(): pl.pallas_call(layer_kernel, name='layer', out_shape=(jax.ShapeDtypeStruc...  412 us

profile of v2, /device:TPU:0, one launch (start us, length us, event | category | flops | bytes accessed | tf_op | source)
XLA Modules:
  0.0 420.2 jit_solution(11699795866743467125)
XLA Ops:
  1.3 412.5 %layer.1 = (bf16[1024,2048]{1,0:T(8,128)(2,1)}, bf16[1024,256]{1,0:T(8,128)(2,1)}, bf16[1024,256]{1,0:T(8,128)(2,1)}, bf16[57,2,8,512,128]{4,3,2,1,0:T(8,128)(2,1)}) custom-call(bf16[1024,2048]{1,0:T(8,128)(2,1)} %bitcast.5, s32[1]{0:T(128)S(6)} %copy.12.plen, f32[1,128]{1,0:T(1,128)} %bitcast.9, bf16[128,18944]{1,0:T(8,128)(2,1)} %w_in.1, ...), custom_call_target="tpu_custom_call" | custom-call | tf_op jit(solution)/shard_map/layer/pallas_call | solution.py:467
  413.7 0.0 copy-start.1
  413.8 0.0 copy-start
  413.8 4.9 %copy.13 = bf16[1,1024,2048]{2,1,0:T(8,128)(2,1)} copy(bf16[1,1024,2048]{2,1,0:T(8,128)(2,1)} %bitcast.6) | data formatting | bytes 8388608
  418.6 0.0 copy-done.1
  418.6 0.8 copy.14
  419.4 0.0 copy-done
  419.4 0.8 copy.15
Async XLA Ops:
  413.7 4.9 %copy-start.1 = (bf16[1024,256]{1,0:T(8,128)(2,1)S(1)}, bf16[1024,256]{1,0:T(8,128)(2,1)}, u32[]{:S(2)}) copy-start(bf16[1024,256]{1,0:T(8,128)(2,1)} %get-tuple-element.7) | copy-start | bytes 1572868
  413.8 5.7 %copy-start = (bf16[1024,256]{1,0:T(8,128)(2,1)S(1)}, bf16[1024,256]{1,0:T(8,128)(2,1)}, u32[]{:S(2)}) copy-start(bf16[1024,256]{1,0:T(8,128)(2,1)} %get-tuple-element.8) | copy-start | bytes 1572868

commit v3 on v2

--- a/solution.py
+++ b/solution.py
@@ -18,12 +18,11 @@
 TRIPLES = 19
 NU = 3 * TRIPLES
 LAST = TRIPLES - 1
-M = 18
+M = 19
 R = NU - M
 LAG = 1
-XLAG = 1
-OFF = 4 * LAG + XLAG + 1
-STEPS = 2 * LAST + OFF + 2
+OFF = 4 * LAG + 1
+STEPS = 2 * LAST + OFF + 1
 DONE = 8
 RB = 256
 
@@ -39,8 +38,8 @@
     return (z * 2 + y) * 2 + c
 
 
-def layer_kernel(x, plen, ln, w_in, w_out, tab, y_out, k_out, v_out, G,
-                 Pv, xv, h, acc, wg, wp, wx, wo, woa, a, q, kk, vv, o, cs, sn, tb, ln_all,
+def layer_kernel(x, plen, ln, w_in, w_out, tab, acc_out, o_out, k_out, v_out, G,
+                 Pv, xv, h, acc, wg, wp, wx, wo, woa, a, u1, q, kk, vv, o, cs, sn, tb, ln_all,
                  pack_sem, own_sem, in_sem, out_sem, ld, rs, rr, xs, xr, ds_, dr, ls, lr):
     pod, d = lax.axis_index("pod"), lax.axis_index("d")
     c, yy, zz = d % 2, (d // 2) % 2, d // 4
@@ -113,6 +112,11 @@
         return pltpu.make_async_remote_copy(src_ref=ln, dst_ref=ln_all.at[d], send_sem=ls.at[t], recv_sem=lr.at[t],
                                             device_id=(pod, (d + t) % 16), device_id_type=MESH)
 
+    def crossed(m):
+        u = 3 * m + 1 - pod
+        cross(m, u, 1, 7).wait_recv()
+        share(u, c).start()
+
     def send_own(s):
         cw(s, 1).start()
         ccw(s, 1).start()
@@ -208,12 +212,14 @@
             p, vv[0:n, :], preferred_element_type=jnp.float32).astype(jnp.bfloat16)
 
     def mlp_in(b, slot):
-        g = proj(b, wg[slot])
-        p = proj(b, wp[slot])
+        mine, other = u1[rows(b), :], proj(b, wp[slot])
+        g, p = jnp.where(pod == 0, mine, other), jnp.where(pod == 0, other, mine)
         a[rows(b), :] = (g * jax.nn.sigmoid(g) * p).astype(jnp.bfloat16)
 
-    def y_copy(b):
-        return pltpu.make_async_copy(xv.at[rows(b), :], y_out.at[rows(b), :], out_sem.at[b])
+    def acc_copy(b):
+        return pltpu.make_async_copy(acc.at[rows(b), :], acc_out.at[rows(b), :], out_sem.at[b])
+
+    o_copy = pltpu.make_async_copy(o, o_out, out_sem.at[6])
 
     k_copy = pltpu.make_async_copy(kk, k_out, out_sem.at[4])
     v_copy = pltpu.make_async_copy(vv, v_out, out_sem.at[5])
@@ -236,7 +242,6 @@
         @pl.when((t >= 2) & (t < LAST))
         def _():
             if b == 0:
-                wait_load(wg.at[slot], ld.at[slot, 0])
                 wait_load(wp.at[slot], ld.at[slot, 1])
             mlp_in(b, slot)
 
@@ -260,7 +265,8 @@
             acc[rows(b), :] += jnp.dot(a[rows(b), :], wo[slot], preferred_element_type=jnp.float32)
 
     def out_attention(b, i, w):
-        return acc[rows(b), :] + jnp.dot(o[rows(b), i * UNIT:(i + 1) * UNIT], w[...], preferred_element_type=jnp.float32)
+        return acc[rows(b), :] + jnp.dot(o[rows(b), pl.ds(pl.multiple_of(i * UNIT, UNIT), UNIT)], w[...],
+                                        preferred_element_type=jnp.float32)
 
     def attention(blocks, t, second):
         @pl.when((t >= 2) & (t < 2 + HEADS // 2))
@@ -276,8 +282,12 @@
 
         @pl.when((t >= 0) & (t < LAST))
         def _():
-            for i in range(3):
-                here(3 * t + i)
+            @pl.when(t < 2)
+            def _():
+                here(3 * t + pod)
+
+            here(3 * t + 1 - pod)
+            here(3 * t + 2)
 
         @pl.when(t == 0)
         def _():
@@ -292,18 +302,12 @@
 
         @pl.when((t >= 2) & (t < LAST))
         def _():
-            load_in(3 * t, wg.at[slot], ld.at[slot, 0])
-            load_in(3 * t + 1, wp.at[slot], ld.at[slot, 1])
+            load_in(3 * t + 1 - pod, wp.at[slot], ld.at[slot, 1])
             load_out(3 * t + 2, wo.at[slot], ld.at[slot, 2])
 
         @pl.when(t == 6)
         def _():
             load_out(5, woa, ld.at[0, 3])
-
-        @pl.when(t == LAST)
-        def _():
-            here(3 * LAST + 1)
-            load_out(3 * LAST + 1, wo.at[LAST % 2], ld.at[LAST % 2, 2])
 
     def step(i, odd):
         is_out = odd == OFF % 2
@@ -313,25 +317,41 @@
         def work(n):
             if is_out:
                 before = jnp.where(i < OFF, -1, t - 1)
+
+                @pl.when((t >= 2) & (t < LAST))
+                def _():
+                    if n == 0:
+                        here(3 * t + pod)
+                        load_in(3 * t + pod, wg.at[slot], ld.at[slot, 0])
+                    if n == 2:
+                        wait_load(wg.at[slot], ld.at[slot, 0])
+                    if n > 1:
+                        for b in (2 * n - 4, 2 * n - 3):
+                            u1[rows(b), :] = proj(b, wg[slot])
+
                 if n < 2:
                     slice_out(2 * n, before, (t + 1) % 2)
                     slice_out(2 * n + 1, before, (t + 1) % 2)
                     if n == 1:
-                        arrive(t)
+                        @pl.when((t >= 0) & (t < LAST))
+                        def _():
+                            crossed(t)
                 elif n == 2:
-                    attention((0, 1, 2), t, 0)
+                    attention((0, 1, 2), t - 1, 1)
 
                     @pl.when(t == LAST)
                     def _():
                         wait_load(woa, ld.at[0, 3])
                         for b in range(4):
-                            acc[rows(b), :] = out_attention(b, 1, woa)
+                            acc[rows(b), :] = out_attention(b, 1 + pod, woa)
+                            if b:
+                                acc_copy(b - 1).start()
                 else:
-                    slice_in(0, t, slot)
-                    attention((3,), t, 0)
+                    attention((3,), t - 1, 1)
+                    arrive(t)
                 return
             if n == 0:
-                @pl.when(i == (2 if OFF % 2 else 3))
+                @pl.when(i == 2)
                 def _():
                     x_in.wait()
                     for j in range(1, 16):
@@ -343,14 +363,17 @@
                     k_copy.start()
                     v_copy.start()
 
-            @pl.when(i == (2 if OFF % 2 else 3))
+                @pl.when(t == 7)
+                def _():
+                    o_copy.start()
+
+            @pl.when(i == 2)
             def _():
                 norm(n)
                 tables(n)
 
-            if n < 3:
-                slice_in(n + 1, t, slot)
-            attention(((0, 1), (2,), (), (3,))[n], t, 1)
+            slice_in(n, t, slot)
+            attention((n,), t, 0)
             if n == 3:
                 @pl.when(t == 6)
                 def _():
@@ -360,8 +383,8 @@
 
                 @pl.when(t == LAST - 1)
                 def _():
-                    here(3 * LAST)
-                    load_out(3 * LAST, woa, ld.at[0, 3])
+                    here(3 * LAST + pod)
+                    load_out(3 * LAST + pod, woa, ld.at[0, 3])
 
         @pl.when(i == 2)
         def _():
@@ -398,14 +421,6 @@
             ccw(s, 4).wait_recv()
             pass_on(s, 4)
 
-        s = i - LAG * 4 - XLAG
-
-        @pl.when((s >= 0) & (s < 2 * M) & (s % 2 == 0))
-        def _():
-            u = 3 * (s // 2) + 1 - pod
-            cross(s // 2, u, 1, 7).wait_recv()
-            share(u, c).start()
-
         work(3)
         s = i - DONE
 
@@ -432,27 +447,72 @@
 
     lax.fori_loop(0, STEPS // 2, two_steps, 0)
 
-    last = LAST % 2
-    wait_load(wo.at[last], ld.at[last, 2])
+    acc_copy(3).start()
+    crossed(LAST)
+    here(3 * LAST + 2)
+    here(3 * LAST + 1 - pod)
+
+    def sent_late(s, _):
+        sent(s)
+        return 0
+
+    lax.fori_loop(STEPS - DONE, R, sent_late, 0)
+    for t in range(1, 16):
+        ln_copy(t).wait_send()
     for b in range(4):
-        if b == 2:
-            here(3 * LAST + 2)
-            load_out(3 * LAST + 2, wo.at[1 - last], ld.at[1 - last, 2])
-        acc[rows(b), :] = out_attention(b, 2, wo.at[last])
-    wait_load(wo.at[1 - last], ld.at[1 - last, 2])
+        acc_copy(b).wait()
+    k_copy.wait()
+    v_copy.wait()
+    o_copy.wait()
+
+
+def finish_kernel(acc, o, k, v, G, y, k_out, v_out, av, ov, wv, yv, kk, vv, in_sem, acc_sem, out_sem):
+    pod, d = lax.axis_index("pod"), lax.axis_index("d")
+    yy, zz = (d // 2) % 2, d // 4
+    r = (1 - yy) * zz + yy * (7 - zz)
+    for at, u in ((0, 3 * LAST + 1 - pod), (UNIT, 3 * LAST + 2)):
+        for cc in range(2):
+            for rel in range(8):
+                src = device_of((r + rel) % 8, cc)
+                pltpu.make_async_copy(G.at[u, cc, rel],
+                                      wv.at[pl.ds(at, UNIT), pl.ds(pl.multiple_of(src * 128, 128), 128)],
+                                      in_sem.at[0]).start()
+    for at, i in ((0, 2 - pod), (UNIT, 3)):
+        pltpu.make_async_copy(o.at[:, pl.ds(pl.multiple_of(i * UNIT, UNIT), UNIT)],
+                              ov.at[:, pl.ds(at, UNIT)], in_sem.at[1]).start()
+    k_in = pltpu.make_async_copy(k, kk, in_sem.at[2])
+    v_in = pltpu.make_async_copy(v, vv, in_sem.at[3])
+    k_copy = pltpu.make_async_copy(kk, k_out, out_sem.at[4])
+    v_copy = pltpu.make_async_copy(vv, v_out, out_sem.at[5])
+
+    def rows(b):
+        return pl.ds(b * RB, RB)
+
+    def acc_in(b):
+        return pltpu.make_async_copy(acc.at[rows(b), :], av.at[rows(b), :], acc_sem.at[b])
+
+    def y_copy(b):
+        return pltpu.make_async_copy(yv.at[rows(b), :], y.at[rows(b), :], out_sem.at[b])
+
+    acc_in(0).start()
+    pltpu.make_async_copy(wv, wv, in_sem.at[0]).wait()
+    for b in range(1, 4):
+        acc_in(b).start()
+    k_in.start()
+    v_in.start()
+    pltpu.make_async_copy(ov, ov, in_sem.at[1]).wait()
     for b in range(4):
-        xv[rows(b), :] = out_attention(b, 3, wo.at[1 - last]).astype(jnp.bfloat16)
+        acc_in(b).wait()
+        if b == 3:
+            k_in.wait()
+            v_in.wait()
+            k_copy.start()
+            v_copy.start()
+        yv[rows(b), :] = (av[rows(b), :] + jnp.dot(ov[rows(b), :], wv[...], preferred_element_type=jnp.float32)
+                          ).astype(jnp.bfloat16)
         if b:
             y_copy(b - 1).start()
     y_copy(3).start()
-
-    def sent_late(s, _):
-        sent(s)
-        return 0
-
-    lax.fori_loop(STEPS - DONE, R, sent_late, 0)
-    for t in range(1, 16):
-        ln_copy(t).wait_send()
     for b in range(4):
         y_copy(b).wait()
     k_copy.wait()
@@ -464,25 +524,37 @@
     anyspace = pl.BlockSpec(memory_space=pl.ANY)
     vmem = pltpu.VMEM
     dma = pltpu.SemaphoreType.DMA
-    return pl.pallas_call(
+    acc, o, k, v, gathered = pl.pallas_call(
         layer_kernel,
         name="layer",
-        out_shape=(jax.ShapeDtypeStruct((T, E), bf), jax.ShapeDtypeStruct((T, HEAD), bf),
+        out_shape=(jax.ShapeDtypeStruct((T, E), f32), jax.ShapeDtypeStruct((T, HEADS * HEAD), bf),
+                   jax.ShapeDtypeStruct((T, HEAD), bf),
                    jax.ShapeDtypeStruct((T, HEAD), bf), jax.ShapeDtypeStruct((NU, 2, 8, UNIT, 128), bf)),
         in_specs=[anyspace, pl.BlockSpec(memory_space=pltpu.SMEM), pl.BlockSpec(memory_space=vmem),
                   anyspace, anyspace, anyspace],
-        out_specs=(anyspace,) * 4,
+        out_specs=(anyspace,) * 5,
         scratch_shapes=[
             vmem((NU, UNIT, 128), bf), vmem((T, E), bf), vmem((T, E), bf), vmem((T, E), f32),
             vmem((2, 2, 8, 128, UNIT), bf), vmem((2, 2, 8, 128, UNIT), bf), vmem((2, 8, 128, UNIT), bf),
-            vmem((2, UNIT, E), bf), vmem((UNIT, E), bf), vmem((T, UNIT), bf),
+            vmem((2, UNIT, E), bf), vmem((UNIT, E), bf), vmem((T, UNIT), bf), vmem((T, UNIT), f32),
             vmem((HEADS, T, HEAD), bf), vmem((T, HEAD), bf), vmem((T, HEAD), bf), vmem((T, HEADS * HEAD), bf),
             vmem((T, 128), f32), vmem((T, 128), f32), vmem((4, 32, 128), f32), vmem((16, 1, 128), f32),
-            dma((2,)), dma, dma((2,)), dma((6,)), dma((2, 4)), dma((R, 8)), dma((R, 8)), dma((M,)), dma((M,)),
+            dma((2,)), dma, dma((2,)), dma((7,)), dma((2, 4)), dma((R, 8)), dma((R, 8)), dma((M,)), dma((M,)),
             dma((NU,)), dma((NU,)), dma((16,)), dma((16,))],
         compiler_params=pltpu.CompilerParams(collective_id=0, has_side_effects=True,
                                              vmem_limit_bytes=63 * 1024 * 1024),
     )(x, plen, ln, w_in, w_out, tab)
+    return pl.pallas_call(
+        finish_kernel,
+        name="finish_layer",
+        out_shape=(jax.ShapeDtypeStruct((T, E), bf), jax.ShapeDtypeStruct((T, HEAD), bf),
+                   jax.ShapeDtypeStruct((T, HEAD), bf)),
+        in_specs=[anyspace] * 5,
+        out_specs=(anyspace,) * 3,
+        scratch_shapes=[vmem((T, E), f32), vmem((T, 2 * UNIT), bf), vmem((2 * UNIT, E), bf), vmem((T, E), bf),
+                        vmem((T, HEAD), bf), vmem((T, HEAD), bf), dma((4,)), dma((4,)), dma((6,))],
+        compiler_params=pltpu.CompilerParams(vmem_limit_bytes=63 * 1024 * 1024),
+    )(acc, o, k, v, gathered)
 
 
 def rope_tables():
@@ -496,7 +568,7 @@
     tab = rope_tables()
 
     def local_layer(x, plen, ln, w_in, w_out):
-        y, k, v, _ = layer(x[0], plen, ln[None], w_in, w_out, tab)
+        y, k, v = layer(x[0], plen, ln[None], w_in, w_out, tab)
         return y[None], k[None], v[None]
 
     return jax.shard_map(local_layer, mesh=mesh,

time: 420 us -> 414 us (0.986)
  local copies, waits for them, and re-layouts: 6.47 us -> 0 us
    pallas_call x1, Pallas kernels: 412 us -> 402 us  [layer(): pl.pallas_call(layer_kernel, name='layer', out_shape=(jax.ShapeDtypeStruc...]
    pallas_call x0 -> x1, Pallas kernels: none -> 10.1 us  [layer(): pl.pallas_call(finish_kernel, name='finish_layer', out_shape=(jax.ShapeDt...]
    unnamed x7 -> x0, local copies, waits for them, and re-layouts: 6.47 us -> none
where the time goes in v3:
time: 414 us; the launch traced here: 413 us
  Pallas kernels  412 us (100%)
    pallas_call x1, Pallas kernels, layer(): pl.pallas_call(layer_kernel, name='layer', out_shape=(jax.ShapeDtypeStruc...  402 us
    pallas_call x1, Pallas kernels, layer(): pl.pallas_call(finish_kernel, name='finish_layer', out_shape=(jax.ShapeDt...  10.1 us

profile of v3, /device:TPU:0, one launch (start us, length us, event | category | flops | bytes accessed | tf_op | source)
XLA Modules:
  0.0 413.4 jit_solution(7092995201419147831)
XLA Ops:
  1.3 401.8 %layer.1 = (f32[1024,2048]{1,0:T(8,128)}, bf16[1024,2048]{1,0:T(8,128)(2,1)}, bf16[1024,256]{1,0:T(8,128)(2,1)}, bf16[1024,256]{1,0:T(8,128)(2,1)}, bf16[57,2,8,512,128]{4,3,2,1,0:T(8,128)(2,1)}) custom-call(bf16[1024,2048]{1,0:T(8,128)(2,1)} %bitcast.5, s32[1]{0:T(128)S(6)} %copy.9.plen, f32[1,128]{1,0:T(1,128)} %bitcast.6, bf16[128,18944]{1,0:T(8,128)(2,1)} %w_in.1, ...), custom_call_target="tpu_custom_call" | custom-call | tf_op jit(solution)/shard_map/layer/pallas_call | solution.py:527
  403.1 10.1 %finish_layer.1 = (bf16[1024,2048]{1,0:T(8,128)(2,1)}, bf16[1024,256]{1,0:T(8,128)(2,1)}, bf16[1024,256]{1,0:T(8,128)(2,1)}) custom-call(f32[1024,2048]{1,0:T(8,128)} %get-tuple-element.11.acc, bf16[1024,2048]{1,0:T(8,128)(2,1)} %get-tuple-element.12.o, bf16[1024,256]{1,0:T(8,128)(2,1)} %get-tuple-element.13.k, bf16[1024,256]{1,0:T(8,128)(2,1)} %get-tuple-element.14.v, ...), custom_call_target="tpu_custom_call" | custom-call | tf_op jit(solution)/shard_map/finish_layer/pallas_call | solution.py:547
